TPU v7x, 32 devices: a whole 2x2x4 slice. The times are simulated.
32 devices in a mesh: dp: 16 (over z, y, x), mp: 2 (over core).
Axes of the slice: x: 2, y: 2, z: 4, core: 2. Of those that a mesh axis runs over, the one named last changes fastest.
Arguments:
- inputs: bfloat16 [2048, 1792], P('dp', 'mp'), may hold values from -6 to 6
- cotangent: bfloat16 [2048, 1792], P('dp', 'mp'), may hold values from -6 to 6
- gate_weight: bfloat16 [9472, 1792], P(('mp', 'dp')), may hold values from -0.125 to 0.125
- up_weight: bfloat16 [9472, 1792], P(('mp', 'dp')), may hold values from -0.125 to 0.125
- down_weight: bfloat16 [9472, 1792], P(('mp', 'dp')), may hold values from -0.0625 to 0.0625
Outputs:
- input_grad: bfloat16 [2048, 1792], P('dp', 'mp')
- gate_grad: bfloat16 [9472, 1792], P(('mp', 'dp'))
All inputs are finite; a program needn't handle non-finite values.
Results may differ from a plain program's by a relative error of at most 0.009.
Values may be sent and summed in bfloat16 or wider, within the bound.
A program may use at most 320 MiB of HBM per device.

v0:
```python
import jax
import jax.numpy as jnp
from jax import lax
from jax.sharding import PartitionSpec as P


def tdot(left, right):
    return lax.dot_general(
        left, right, (((0,), (0,)), ((), ())), preferred_element_type=jnp.float32
    )


def rdot(left, right):
    return lax.dot_general(
        left, right, (((1,), (1,)), ((), ())), preferred_element_type=jnp.float32
    )


def per_device(inputs, cotangent, gate_weight, up_weight, down_weight):

    def tokens(block):
        rows = lax.all_gather(block, "dp", axis=0, tiled=True)
        return lax.all_gather(rows, "mp", axis=1, tiled=True)

    full_in = tokens(inputs)
    full_cot = tokens(cotangent)
    gate = rdot(full_in, gate_weight)
    up = rdot(full_in, up_weight)
    dhidden = rdot(full_cot, down_weight)
    sig = jax.nn.sigmoid(gate)
    act = gate * sig
    dup = (dhidden * act).astype(jnp.bfloat16)
    dgate = (dhidden * up * sig * (1.0 + gate * (1.0 - sig))).astype(jnp.bfloat16)
    partial = jnp.dot(dgate, gate_weight, preferred_element_type=jnp.float32)
    partial = partial + jnp.dot(dup, up_weight, preferred_element_type=jnp.float32)
    partial = lax.psum_scatter(partial.astype(jnp.bfloat16), "mp", scatter_dimension=1, tiled=True)
    input_grad = lax.psum_scatter(partial, "dp", scatter_dimension=0, tiled=True)
    gate_grad = tdot(dgate, full_in).astype(jnp.bfloat16)
    return (input_grad, gate_grad)


def solution(mesh):
    placed = (
        P("dp", "mp"),
        P("dp", "mp"),
        P(("mp", "dp"), None),
        P(("mp", "dp"), None),
        P(("mp", "dp"), None),
    )
    return jax.shard_map(
        per_device,
        mesh=mesh,
        in_specs=placed,
        out_specs=(P("dp", "mp"), P(("mp", "dp"), None)),
        check_vma=False,
    )
```

profile of v0, /device:TPU:0, one launch (start us, length us, event | category | flops | bytes accessed | tf_op | source)
XLA Modules:
  0.0 350.5 jit_solution(10456565937666532263)
XLA Ops:
  7.2 0.0 copy-start
  7.2 0.0 all-gather.5.cloned.1.call-start
  7.2 0.7 all-gather.5.cloned.1.call-update
  7.9 0.0 all-gather.9.cloned.1.call-start
  8.0 0.7 all-gather.9.cloned.1.call-update
  8.7 0.0 all-gather.7.cloned.1.call-start
  8.7 76.4 %all-gather.5.cloned.1.call-done = bf16[2048,896]{1,0:T(8,128)(2,1)} async-done(((bf16[128,896]{1,0:T(8,128)(2,1)}), bf16[2048,896]{1,0:T(8,128)(2,1)}) %all-gather.5.cloned.1.call-update) | async-done | bytes 3670032 | tf_op jit(solution)/shard_map/all_gather | solution.py:22
  85.1 0.0 all-gather.7.cloned.1.call-update
  85.1 0.0 all-gather.11.cloned.1.call-start
  85.2 72.9 %all-gather.9.cloned.1.call-done = bf16[2048,896]{1,0:T(8,128)(2,1)} async-done(((bf16[128,896]{1,0:T(8,128)(2,1)}), bf16[2048,896]{1,0:T(8,128)(2,1)}) %all-gather.9.cloned.1.call-update) | async-done | bytes 3670032 | tf_op jit(solution)/shard_map/all_gather | solution.py:22
  158.1 0.0 all-gather.11.cloned.1.call-update
  158.1 0.0 reduce-scatter.7.cloned.1.call-start
  158.1 18.3 %all-gather.7.cloned.1.call-done = bf16[2048,1792]{1,0:T(8,128)(2,1)} async-done(((bf16[2048,896]{1,0:T(8,128)(2,1)}), bf16[2048,1792]{1,0:T(8,128)(2,1)}) %all-gather.7.cloned.1.call-update) | async-done | bytes 7340048 | tf_op jit(solution)/shard_map/all_gather | solution.py:23
  176.4 5.7 %fusion.5 = f32[2048,296]{0,1:T(8,128)S(1)} fusion(bf16[2048,1792]{1,0:T(8,128)(2,1)} %all-gather.7.cloned.1.call-done, bf16[296,1792]{1,0:T(8,128)(2,1)} %param.9), kind=kOutput, calls=%fused_computation.10 | convolution fusion | flops 2172649472 | bytes 10825728 | tf_op jit(solution)/shard_map/dot_general | solution.py:14
  182.1 15.1 %all-gather.11.cloned.1.call-done = bf16[2048,1792]{1,0:T(8,128)(2,1)} async-done(((bf16[2048,896]{1,0:T(8,128)(2,1)}), bf16[2048,1792]{1,0:T(8,128)(2,1)}) %all-gather.11.cloned.1.call-update) | async-done | bytes 7340048 | tf_op jit(solution)/shard_map/all_gather | solution.py:23
  197.2 0.0 copy-done
  197.2 0.0 copy-start.4
  197.2 0.0 copy-start.5
  197.2 5.6 %fusion.6 = f32[2048,296]{0,1:T(8,128)S(1)} fusion(bf16[2048,1792]{1,0:T(8,128)(2,1)} %all-gather.11.cloned.1.call-done, bf16[296,1792]{1,0:T(8,128)(2,1)S(1)} %copy-done), kind=kOutput, calls=%fused_computation.11 | convolution fusion | flops 2172649472 | bytes 10825728 | tf_op jit(solution)/shard_map/dot_general | solution.py:14
  202.9 0.0 copy-done.4
  202.9 0.0 copy-done.5
  202.9 2.8 fusion.2
  205.7 0.0 copy-start.2
  205.7 7.4 %fusion.7 = f32[2048,1792]{1,0:T(8,128)} fusion(bf16[2048,296]{0,1:T(8,128)(2,1)S(1)} %fusion.2, bf16[296,1792]{1,0:T(8,128)(2,1)S(1)} %copy-done), kind=kOutput, calls=%fused_computation.12 | convolution fusion | flops 2172649472 | bytes 16953344 | tf_op jit(solution)/shard_map/dot_general | solution.py:34
  213.1 0.0 copy-done.2
  213.1 9.3 %add_convert_fusion = bf16[2048,1792]{1,0:T(8,128)(2,1)} fusion(f32[2048,1792]{1,0:T(8,128)} %fusion.7, bf16[296,1792]{1,0:T(8,128)(2,1)S(1)} %copy-done.4, f32[2048,296]{0,1:T(8,128)S(1)} %fusion.5, f32[2048,296]{0,1:T(8,128)S(1)} %fusion.6), kind=kOutput, calls=%fused_computation | convolution fusion | flops 2183626752 | bytes 27930624 | tf_op jit(solution)/shard_map/dot_general | solution.py:35
  222.4 10.5 %copy.7 = bf16[2048,1792]{0,1:T(8,128)(2,1)} copy(bf16[2048,1792]{1,0:T(8,128)(2,1)} %add_convert_fusion) | data formatting | bytes 14680064
  232.9 0.0 reduce-scatter.7.cloned.1.call-update
  232.9 0.0 reduce-scatter.5.cloned.1.call-start
  233.0 17.4 %reduce-scatter.7.cloned.1.call-done = bf16[896,2048]{1,0:T(8,128)(2,1)} async-done(((bf16[1792,2048]{1,0:T(8,128)(2,1)}), bf16[896,2048]{1,0:T(8,128)(2,1)}) %reduce-scatter.7.cloned.1.call-update) | async-done | bytes 3670032
  250.4 6.1 %copy.8 = bf16[2048,896]{1,0:T(8,128)(2,1)} copy(bf16[2048,896]{0,1:T(8,128)(2,1)} %bitcast.14) | data formatting | bytes 7340032
  256.5 0.0 copy-start.3
  256.5 0.0 reduce-scatter.5.cloned.1.call-update
  256.5 1.3 copy-done.3
  257.8 0.0 copy-start.1
  257.8 6.5 %convolution_convert_fusion = bf16[296,1792]{1,0:T(8,128)(2,1)} fusion(bf16[2048,296]{0,1:T(8,128)(2,1)S(1)} %copy-done.3, bf16[2048,1792]{1,0:T(8,128)(2,1)} %all-gather.11.cloned.1.call-done), kind=kOutput, calls=%fused_computation.5 | convolution fusion | flops 2173179904 | bytes 9613312 | tf_op jit(solution)/shard_map/dot_general | solution.py:8
  264.3 79.3 %reduce-scatter.5.cloned.1.call-done = bf16[128,896]{1,0:T(8,128)(2,1)} async-done(((bf16[2048,896]{1,0:T(8,128)(2,1)}), bf16[128,896]{1,0:T(8,128)(2,1)}) %reduce-scatter.5.cloned.1.call-update) | async-done | bytes 229392 | tf_op jit(solution)/shard_map/reduce_scatter | solution.py:37
  343.6 0.0 copy-done.1
Async XLA Ops:
  7.2 190.1 %copy-start = (bf16[296,1792]{1,0:T(8,128)(2,1)S(1)}, bf16[296,1792]{1,0:T(8,128)(2,1)}, u32[]{:S(2)}) copy-start(bf16[296,1792]{1,0:T(8,128)(2,1)} %param.7) | copy-start | bytes 3182596
  7.2 77.9 %all-gather.5.cloned.1.call-start = ((), (), s32[]{:S(2)}) async-start(), calls=%async_computation.2 | async-start | bytes 3899392 | tf_op jit(solution)/shard_map/all_gather | solution.py:22
  7.9 150.2 %all-gather.9.cloned.1.call-start = ((), (), s32[]{:S(2)}) async-start(), calls=%async_computation.4 | async-start | bytes 3899392 | tf_op jit(solution)/shard_map/all_gather | solution.py:22
  8.7 167.7 %all-gather.7.cloned.1.call-start = ((), (), s32[]{:S(2)}) async-start(), calls=%async_computation.3 | async-start | bytes 11010048 | tf_op jit(solution)/shard_map/all_gather | solution.py:23
  85.1 112.1 %all-gather.11.cloned.1.call-start = ((), (), s32[]{:S(2)}) async-start(), calls=%async_computation.5 | async-start | bytes 11010048 | tf_op jit(solution)/shard_map/all_gather | solution.py:23
  158.1 92.3 %reduce-scatter.7.cloned.1.call-start = ((), (), s32[]{:S(2)}) async-start(), calls=%async_computation.7 | async-start | bytes 11010048
  197.2 5.6 %copy-start.4 = (bf16[296,1792]{1,0:T(8,128)(2,1)S(1)}, bf16[296,1792]{1,0:T(8,128)(2,1)}, u32[]{:S(2)}) copy-start(bf16[296,1792]{1,0:T(8,128)(2,1)} %param.8) | copy-start | bytes 3182596
  197.2 5.6 %copy-start.5 = (bf16[2048,1792]{1,0:T(8,128)(2,1)S(1)}, bf16[2048,1792]{1,0:T(8,128)(2,1)}, u32[]{:S(2)}) copy-start(bf16[2048,1792]{1,0:T(8,128)(2,1)} %all-gather.11.cloned.1.call-done) | copy-start | bytes 22020100
  205.7 7.4 %copy-start.2 = (bf16[2048,296]{0,1:T(8,128)(2,1)}, bf16[2048,296]{0,1:T(8,128)(2,1)S(1)}, u32[]{:S(2)}) copy-start(bf16[2048,296]{0,1:T(8,128)(2,1)S(1)} %fusion.2) | copy-start | bytes 3637252
  232.9 110.7 %reduce-scatter.5.cloned.1.call-start = ((), (), s32[]{:S(2)}) async-start(), calls=%async_computation.6 | async-start | bytes 3899392 | tf_op jit(solution)/shard_map/reduce_scatter | solution.py:37
  256.5 1.3 copy-start.3
  257.8 85.9 %copy-start.1 = (bf16[296,1792]{1,0:T(8,128)(2,1)S(1)}, bf16[296,1792]{1,0:T(8,128)(2,1)}, u32[]{:S(2)}) copy-start(bf16[296,1792]{1,0:T(8,128)(2,1)} %param.7) | copy-start | bytes 3182596
Sparse Core Ops, SparseCore 0:
  10.7 74.3 all-gather.4
  87.9 70.1 all-gather.8
  159.6 16.7 all-gather.6
  177.8 19.3 all-gather.10
  233.0 17.3 reduce-scatter.6
  256.6 86.9 reduce-scatter.4
where the time goes:
time: 351 us; the launch traced here: 350 us
  waiting for transfers between devices  281 us (80%)
  matrix products  37.3 us (11%)
  local copies, waits for them, and re-layouts  17.9 us (5%)
  between operations  14.2 us (4%)
    all_gather x2, waiting for transfers between devices, tokens(): rows = lax.all_gather(block, 'dp', axis=0, tiled=True)  149 us
    reduce_scatter x1, waiting for transfers between devices, per_device(): lax.psum_scatter(partial, 'dp', scatter_dimension=0, tiled=True)  79.3 us
    all_gather x2, waiting for transfers between devices, tokens(): return lax.all_gather(rows, 'mp', axis=1, tiled=True)  33.4 us
    unnamed x7, waiting for transfers between devices  18.9 us
    unnamed x14, local copies, waits for them, and re-layouts  17.9 us
    dot_general x3, matrix products, rdot(): lax.dot_general(left, right, (((1,), (1,)), ((), ())), preferred_element_...  14.2 us
    dot_general x1, matrix products, per_device(): jnp.dot(dup, up_weight, preferred_element_type=jnp.float32)  9.27 us
    dot_general x1, matrix products, per_device(): partial = jnp.dot(dgate, gate_weight, preferred_element_type=jnp.float32)  7.38 us
  transfers between devices with their start and end apart: 6, of which 6 were waited for; matrix products, arithmetic and copies ran while one was open for 3% of the time, Pallas kernels for 0%

commit v1 on v0

--- a/solution.py
+++ b/solution.py
@@ -19,7 +19,14 @@
 def per_device(inputs, cotangent, gate_weight, up_weight, down_weight):
 
     def tokens(block):
-        rows = lax.all_gather(block, "dp", axis=0, tiled=True)
+        ring = [block]
+        for hop in range(15):
+            ring.append(lax.ppermute(ring[-1], "dp", [(dev, (dev + 1) % 16) for dev in range(16)]))
+        rows = jnp.roll(
+            jnp.concatenate(ring[::-1], axis=0),
+            (lax.axis_index("dp") + 1) * ring[0].shape[0],
+            axis=0,
+        )
         return lax.all_gather(rows, "mp", axis=1, tiled=True)
 
     full_in = tokens(inputs)

time: 351 us -> 510 us (1.45)
  waiting for transfers between devices: 281 us -> 411 us
  other arithmetic: 0 us -> 14.4 us
  local copies, waits for them, and re-layouts: 17.9 us -> 28 us
    ppermute x0 -> x30, waiting for transfers between devices: none -> 307 us  [tokens(): lax.ppermute(ring[-1], 'dp', [(dev, (dev + 1) % 16) for dev in range(16)])]
    all_gather x2 -> x0, waiting for transfers between devices: 149 us -> none  [tokens(): rows = lax.all_gather(block, 'dp', axis=0, tiled=True)]
    all_gather x2, waiting for transfers between devices: 33.4 us -> 7.26 us  [tokens(): return lax.all_gather(rows, 'mp', axis=1, tiled=True)]
    concatenate x0 -> x2, other arithmetic: none -> 14.4 us  [tokens(): jnp.roll(jnp.concatenate(ring[::-1], axis=0), (lax.axis_index('dp') + 1)...]
    unnamed x14 -> x56, local copies, waits for them, and re-layouts: 17.9 us -> 27.9 us
    unnamed x7 -> x5, waiting for transfers between devices: 18.9 us -> 17.5 us
  transfers between devices with their start and end apart: 6 -> 34, of which waited for: 6 -> 33; matrix products, arithmetic and copies ran while one was open for 3% -> 4% of each run, Pallas kernels for 0% -> 0%
where the time goes in v1:
time: 510 us
  waiting for transfers between devices  411 us (81%)
  matrix products  38.4 us (8%)
  local copies, waits for them, and re-layouts  28 us (5%)
  other arithmetic  14.4 us (3%)
  between operations  14.1 us (3%)
    ppermute x30, waiting for transfers between devices, tokens(): lax.ppermute(ring[-1], 'dp', [(dev, (dev + 1) % 16) for dev in range(16)])  307 us
    reduce_scatter x1, waiting for transfers between devices, per_device(): lax.psum_scatter(partial, 'dp', scatter_dimension=0, tiled=True)  79.4 us
    unnamed x56, local copies, waits for them, and re-layouts  27.9 us
    unnamed x5, waiting for transfers between devices  17.5 us
    dot_general x3, matrix products, rdot(): lax.dot_general(left, right, (((1,), (1,)), ((), ())), preferred_element_...  15.1 us
    concatenate x2, other arithmetic, tokens(): jnp.roll(jnp.concatenate(ring[::-1], axis=0), (lax.axis_index('dp') + 1)...  14.4 us
  transfers between devices with their start and end apart: 34, of which 33 were waited for; matrix products, arithmetic and copies ran while one was open for 4% of the time, Pallas kernels for 0%

profile of v1, /device:TPU:0, one launch (start us, length us, event | category | flops | bytes accessed | tf_op | source)
XLA Modules:
  0.0 509.7 jit_solution(5478497158257263812)
XLA Ops:
  7.2 3.0 collective-permute-start
  10.3 9.8 %collective-permute-done = bf16[128,896]{1,0:T(8,128)(2,1)S(1)} collective-permute-done((bf16[128,896]{1,0:T(8,128)(2,1)}, bf16[128,896]{1,0:T(8,128)(2,1)S(1)}, u32[]{:S(2)}, u32[]{:S(2)}) %collective-permute-start) | collective-permute-done | bytes 229408 | tf_op jit(solution)/shard_map/ppermute | solution.py:24
  20.1 10.4 %collective-permute-done.1 = bf16[128,896]{1,0:T(8,128)(2,1)S(1)} collective-permute-done((bf16[128,896]{1,0:T(8,128)(2,1)S(1)}, bf16[128,896]{1,0:T(8,128)(2,1)S(1)}, u32[]{:S(2)}, u32[]{:S(2)}) %collective-permute-start.1) | collective-permute-done | bytes 229408 | tf_op jit(solution)/shard_map/ppermute | solution.py:24
  30.4 9.6 %collective-permute-done.2 = bf16[128,896]{1,0:T(8,128)(2,1)S(1)} collective-permute-done((bf16[128,896]{1,0:T(8,128)(2,1)S(1)}, bf16[128,896]{1,0:T(8,128)(2,1)S(1)}, u32[]{:S(2)}, u32[]{:S(2)}) %collective-permute-start.2) | collective-permute-done | bytes 229408 | tf_op jit(solution)/shard_map/ppermute | solution.py:24
  40.0 9.6 %collective-permute-done.3 = bf16[128,896]{1,0:T(8,128)(2,1)S(1)} collective-permute-done((bf16[128,896]{1,0:T(8,128)(2,1)S(1)}, bf16[128,896]{1,0:T(8,128)(2,1)S(1)}, u32[]{:S(2)}, u32[]{:S(2)}) %collective-permute-start.3) | collective-permute-done | bytes 229408 | tf_op jit(solution)/shard_map/ppermute | solution.py:24
  49.7 9.6 %collective-permute-done.4 = bf16[128,896]{1,0:T(8,128)(2,1)S(1)} collective-permute-done((bf16[128,896]{1,0:T(8,128)(2,1)S(1)}, bf16[128,896]{1,0:T(8,128)(2,1)S(1)}, u32[]{:S(2)}, u32[]{:S(2)}) %collective-permute-start.4) | collective-permute-done | bytes 229408 | tf_op jit(solution)/shard_map/ppermute | solution.py:24
  59.3 9.6 %collective-permute-done.5 = bf16[128,896]{1,0:T(8,128)(2,1)S(1)} collective-permute-done((bf16[128,896]{1,0:T(8,128)(2,1)S(1)}, bf16[128,896]{1,0:T(8,128)(2,1)S(1)}, u32[]{:S(2)}, u32[]{:S(2)}) %collective-permute-start.5) | collective-permute-done | bytes 229408 | tf_op jit(solution)/shard_map/ppermute | solution.py:24
  68.9 10.8 %collective-permute-done.6 = bf16[128,896]{1,0:T(8,128)(2,1)S(1)} collective-permute-done((bf16[128,896]{1,0:T(8,128)(2,1)S(1)}, bf16[128,896]{1,0:T(8,128)(2,1)S(1)}, u32[]{:S(2)}, u32[]{:S(2)}) %collective-permute-start.6) | collective-permute-done | bytes 229408 | tf_op jit(solution)/shard_map/ppermute | solution.py:24
  79.7 11.9 %collective-permute-done.7 = bf16[128,896]{1,0:T(8,128)(2,1)S(1)} collective-permute-done((bf16[128,896]{1,0:T(8,128)(2,1)S(1)}, bf16[128,896]{1,0:T(8,128)(2,1)S(1)}, u32[]{:S(2)}, u32[]{:S(2)}) %collective-permute-start.7) | collective-permute-done | bytes 229408 | tf_op jit(solution)/shard_map/ppermute | solution.py:24
  91.6 11.2 %collective-permute-done.8 = bf16[128,896]{1,0:T(8,128)(2,1)S(1)} collective-permute-done((bf16[128,896]{1,0:T(8,128)(2,1)S(1)}, bf16[128,896]{1,0:T(8,128)(2,1)S(1)}, u32[]{:S(2)}, u32[]{:S(2)}) %collective-permute-start.8) | collective-permute-done | bytes 229408 | tf_op jit(solution)/shard_map/ppermute | solution.py:24
  102.8 11.1 %collective-permute-done.9 = bf16[128,896]{1,0:T(8,128)(2,1)S(1)} collective-permute-done((bf16[128,896]{1,0:T(8,128)(2,1)S(1)}, bf16[128,896]{1,0:T(8,128)(2,1)S(1)}, u32[]{:S(2)}, u32[]{:S(2)}) %collective-permute-start.9) | collective-permute-done | bytes 229408 | tf_op jit(solution)/shard_map/ppermute | solution.py:24
  114.6 10.2 %collective-permute-done.10 = bf16[128,896]{1,0:T(8,128)(2,1)S(1)} collective-permute-done((bf16[128,896]{1,0:T(8,128)(2,1)S(1)}, bf16[128,896]{1,0:T(8,128)(2,1)S(1)}, u32[]{:S(2)}, u32[]{:S(2)}) %collective-permute-start.10) | collective-permute-done | bytes 229408 | tf_op jit(solution)/shard_map/ppermute | solution.py:24
  125.5 9.6 %collective-permute-done.11 = bf16[128,896]{1,0:T(8,128)(2,1)S(1)} collective-permute-done((bf16[128,896]{1,0:T(8,128)(2,1)S(1)}, bf16[128,896]{1,0:T(8,128)(2,1)S(1)}, u32[]{:S(2)}, u32[]{:S(2)}) %collective-permute-start.11) | collective-permute-done | bytes 229408 | tf_op jit(solution)/shard_map/ppermute | solution.py:24
  135.8 9.6 %collective-permute-done.12 = bf16[128,896]{1,0:T(8,128)(2,1)S(1)} collective-permute-done((bf16[128,896]{1,0:T(8,128)(2,1)S(1)}, bf16[128,896]{1,0:T(8,128)(2,1)S(1)}, u32[]{:S(2)}, u32[]{:S(2)}) %collective-permute-start.12) | collective-permute-done | bytes 229408 | tf_op jit(solution)/shard_map/ppermute | solution.py:24
  146.1 9.7 %collective-permute-done.13 = bf16[128,896]{1,0:T(8,128)(2,1)} collective-permute-done((bf16[128,896]{1,0:T(8,128)(2,1)S(1)}, bf16[128,896]{1,0:T(8,128)(2,1)}, u32[]{:S(2)}, u32[]{:S(2)}) %collective-permute-start.13) | collective-permute-done | bytes 229408 | tf_op jit(solution)/shard_map/ppermute | solution.py:24
  155.8 9.9 %collective-permute-done.14 = bf16[128,896]{1,0:T(8,128)(2,1)} collective-permute-done((bf16[128,896]{1,0:T(8,128)(2,1)}, bf16[128,896]{1,0:T(8,128)(2,1)}, u32[]{:S(2)}, u32[]{:S(2)}) %collective-permute-start.14) | collective-permute-done | bytes 229408 | tf_op jit(solution)/shard_map/ppermute | solution.py:24
  167.7 1.0 constant_dynamic-update-slice_fusion.13
  168.7 1.0 constant_dynamic-update-slice_fusion.12
  169.6 1.0 constant_dynamic-update-slice_fusion.11
  171.9 7.2 %fusion.1 = bf16[2048,896]{1,0:T(8,128)(2,1)} fusion(s32[]{:T(128)S(6)} %select_n.13, bf16[2048,896]{1,0:T(8,128)(2,1)S(1)} %constant_dynamic-update-slice_fusion), kind=kLoop, calls=%fused_computation.6 | loop fusion | flops 7340032 | bytes 7340036 | tf_op jit(solution)/shard_map/jit(_roll_dynamic)/concatenate | solution.py:25
  180.1 11.6 %collective-permute-done.15 = bf16[128,896]{1,0:T(8,128)(2,1)S(1)} collective-permute-done((bf16[128,896]{1,0:T(8,128)(2,1)S(1)}, bf16[128,896]{1,0:T(8,128)(2,1)S(1)}, u32[]{:S(2)}, u32[]{:S(2)}) %collective-permute-start.15) | collective-permute-done | bytes 229408 | tf_op jit(solution)/shard_map/ppermute | solution.py:24
  191.7 11.4 %collective-permute-done.16 = bf16[128,896]{1,0:T(8,128)(2,1)S(1)} collective-permute-done((bf16[128,896]{1,0:T(8,128)(2,1)S(1)}, bf16[128,896]{1,0:T(8,128)(2,1)S(1)}, u32[]{:S(2)}, u32[]{:S(2)}) %collective-permute-start.16) | collective-permute-done | bytes 229408 | tf_op jit(solution)/shard_map/ppermute | solution.py:24
  203.1 10.5 %collective-permute-done.17 = bf16[128,896]{1,0:T(8,128)(2,1)S(1)} collective-permute-done((bf16[128,896]{1,0:T(8,128)(2,1)S(1)}, bf16[128,896]{1,0:T(8,128)(2,1)S(1)}, u32[]{:S(2)}, u32[]{:S(2)}) %collective-permute-start.17) | collective-permute-done | bytes 229408 | tf_op jit(solution)/shard_map/ppermute | solution.py:24
  213.6 9.7 %collective-permute-done.18 = bf16[128,896]{1,0:T(8,128)(2,1)S(1)} collective-permute-done((bf16[128,896]{1,0:T(8,128)(2,1)S(1)}, bf16[128,896]{1,0:T(8,128)(2,1)S(1)}, u32[]{:S(2)}, u32[]{:S(2)}) %collective-permute-start.18) | collective-permute-done | bytes 229408 | tf_op jit(solution)/shard_map/ppermute | solution.py:24
  223.2 9.6 %collective-permute-done.19 = bf16[128,896]{1,0:T(8,128)(2,1)S(1)} collective-permute-done((bf16[128,896]{1,0:T(8,128)(2,1)S(1)}, bf16[128,896]{1,0:T(8,128)(2,1)S(1)}, u32[]{:S(2)}, u32[]{:S(2)}) %collective-permute-start.19) | collective-permute-done | bytes 229408 | tf_op jit(solution)/shard_map/ppermute | solution.py:24
  232.8 9.6 %collective-permute-done.20 = bf16[128,896]{1,0:T(8,128)(2,1)S(1)} collective-permute-done((bf16[128,896]{1,0:T(8,128)(2,1)S(1)}, bf16[128,896]{1,0:T(8,128)(2,1)S(1)}, u32[]{:S(2)}, u32[]{:S(2)}) %collective-permute-start.20) | collective-permute-done | bytes 229408 | tf_op jit(solution)/shard_map/ppermute | solution.py:24
  242.5 9.6 %collective-permute-done.21 = bf16[128,896]{1,0:T(8,128)(2,1)S(1)} collective-permute-done((bf16[128,896]{1,0:T(8,128)(2,1)S(1)}, bf16[128,896]{1,0:T(8,128)(2,1)S(1)}, u32[]{:S(2)}, u32[]{:S(2)}) %collective-permute-start.21) | collective-permute-done | bytes 229408 | tf_op jit(solution)/shard_map/ppermute | solution.py:24
  252.1 10.3 %collective-permute-done.22 = bf16[128,896]{1,0:T(8,128)(2,1)S(1)} collective-permute-done((bf16[128,896]{1,0:T(8,128)(2,1)S(1)}, bf16[128,896]{1,0:T(8,128)(2,1)S(1)}, u32[]{:S(2)}, u32[]{:S(2)}) %collective-permute-start.22) | collective-permute-done | bytes 229408 | tf_op jit(solution)/shard_map/ppermute | solution.py:24
  262.4 11.5 %collective-permute-done.23 = bf16[128,896]{1,0:T(8,128)(2,1)S(1)} collective-permute-done((bf16[128,896]{1,0:T(8,128)(2,1)S(1)}, bf16[128,896]{1,0:T(8,128)(2,1)S(1)}, u32[]{:S(2)}, u32[]{:S(2)}) %collective-permute-start.23) | collective-permute-done | bytes 229408 | tf_op jit(solution)/shard_map/ppermute | solution.py:24
  273.9 11.5 %collective-permute-done.24 = bf16[128,896]{1,0:T(8,128)(2,1)S(1)} collective-permute-done((bf16[128,896]{1,0:T(8,128)(2,1)S(1)}, bf16[128,896]{1,0:T(8,128)(2,1)S(1)}, u32[]{:S(2)}, u32[]{:S(2)}) %collective-permute-start.24) | collective-permute-done | bytes 229408 | tf_op jit(solution)/shard_map/ppermute | solution.py:24
  285.4 10.7 %collective-permute-done.25 = bf16[128,896]{1,0:T(8,128)(2,1)S(1)} collective-permute-done((bf16[128,896]{1,0:T(8,128)(2,1)S(1)}, bf16[128,896]{1,0:T(8,128)(2,1)S(1)}, u32[]{:S(2)}, u32[]{:S(2)}) %collective-permute-start.25) | collective-permute-done | bytes 229408 | tf_op jit(solution)/shard_map/ppermute | solution.py:24
  296.1 9.8 %collective-permute-done.26 = bf16[128,896]{1,0:T(8,128)(2,1)S(1)} collective-permute-done((bf16[128,896]{1,0:T(8,128)(2,1)S(1)}, bf16[128,896]{1,0:T(8,128)(2,1)S(1)}, u32[]{:S(2)}, u32[]{:S(2)}) %collective-permute-start.26) | collective-permute-done | bytes 229408 | tf_op jit(solution)/shard_map/ppermute | solution.py:24
  305.9 9.6 %collective-permute-done.27 = bf16[128,896]{1,0:T(8,128)(2,1)S(1)} collective-permute-done((bf16[128,896]{1,0:T(8,128)(2,1)S(1)}, bf16[128,896]{1,0:T(8,128)(2,1)S(1)}, u32[]{:S(2)}, u32[]{:S(2)}) %collective-permute-start.27) | collective-permute-done | bytes 229408 | tf_op jit(solution)/shard_map/ppermute | solution.py:24
  315.5 9.6 %collective-permute-done.28 = bf16[128,896]{1,0:T(8,128)(2,1)S(1)} collective-permute-done((bf16[128,896]{1,0:T(8,128)(2,1)S(1)}, bf16[128,896]{1,0:T(8,128)(2,1)S(1)}, u32[]{:S(2)}, u32[]{:S(2)}) %collective-permute-start.28) | collective-permute-done | bytes 229408 | tf_op jit(solution)/shard_map/ppermute | solution.py:24
  325.1 9.6 %collective-permute-done.29 = bf16[128,896]{1,0:T(8,128)(2,1)S(1)} collective-permute-done((bf16[128,896]{1,0:T(8,128)(2,1)S(1)}, bf16[128,896]{1,0:T(8,128)(2,1)S(1)}, u32[]{:S(2)}, u32[]{:S(2)}) %collective-permute-start.29) | collective-permute-done | bytes 229408 | tf_op jit(solution)/shard_map/ppermute | solution.py:24
  335.3 7.2 %fusion = bf16[2048,896]{1,0:T(8,128)(2,1)} fusion(s32[]{:T(128)S(6)} %select_n.13, bf16[2048,896]{1,0:T(8,128)(2,1)S(1)} %constant_dynamic-update-slice_fusion.16), kind=kLoop, calls=%fused_computation.5 | loop fusion | flops 7340032 | bytes 7340036 | tf_op jit(solution)/shard_map/jit(_roll_dynamic)/concatenate | solution.py:25
  342.8 6.7 %fusion.7 = f32[2048,296]{0,1:T(8,128)S(1)} fusion(bf16[2048,1792]{1,0:T(8,128)(2,1)} %all-gather.3.cloned.1.call-done, bf16[296,1792]{1,0:T(8,128)(2,1)} %param.11), kind=kOutput, calls=%fused_computation.48 | convolution fusion | flops 2172649472 | bytes 10825728 | tf_op jit(solution)/shard_map/dot_general | solution.py:14
  349.5 7.2 %all-gather.5.cloned.1.call-done = bf16[2048,1792]{1,0:T(8,128)(2,1)} async-done(((bf16[2048,896]{1,0:T(8,128)(2,1)}), bf16[2048,1792]{1,0:T(8,128)(2,1)}) %all-gather.5.cloned.1.call-update) | async-done | bytes 7340048 | tf_op jit(solution)/shard_map/all_gather | solution.py:30
  356.7 5.6 %fusion.8 = f32[2048,296]{0,1:T(8,128)S(1)} fusion(bf16[2048,1792]{1,0:T(8,128)(2,1)} %all-gather.5.cloned.1.call-done, bf16[296,1792]{1,0:T(8,128)(2,1)S(1)} %copy-done), kind=kOutput, calls=%fused_computation.49 | convolution fusion | flops 2172649472 | bytes 10825728 | tf_op jit(solution)/shard_map/dot_general | solution.py:14
  362.4 2.8 fusion.4
  365.2 7.4 %fusion.9 = f32[2048,1792]{1,0:T(8,128)} fusion(bf16[2048,296]{0,1:T(8,128)(2,1)S(1)} %fusion.4, bf16[296,1792]{1,0:T(8,128)(2,1)S(1)} %copy-done), kind=kOutput, calls=%fused_computation.50 | convolution fusion | flops 2172649472 | bytes 16953344 | tf_op jit(solution)/shard_map/dot_general | solution.py:41
  372.6 9.4 %add_convert_fusion = bf16[2048,1792]{1,0:T(8,128)(2,1)} fusion(f32[2048,1792]{1,0:T(8,128)} %fusion.9, bf16[296,1792]{1,0:T(8,128)(2,1)S(1)} %copy-done.4, f32[2048,296]{0,1:T(8,128)S(1)} %fusion.7, f32[2048,296]{0,1:T(8,128)S(1)} %fusion.8), kind=kOutput, calls=%fused_computation | convolution fusion | flops 2183626752 | bytes 27930624 | tf_op jit(solution)/shard_map/dot_general | solution.py:42
  382.0 10.5 %copy.7 = bf16[2048,1792]{0,1:T(8,128)(2,1)} copy(bf16[2048,1792]{1,0:T(8,128)(2,1)} %add_convert_fusion) | data formatting | bytes 14680064
  392.6 17.4 %reduce-scatter.7.cloned.1.call-done = bf16[896,2048]{1,0:T(8,128)(2,1)} async-done(((bf16[1792,2048]{1,0:T(8,128)(2,1)}), bf16[896,2048]{1,0:T(8,128)(2,1)}) %reduce-scatter.7.cloned.1.call-update) | async-done | bytes 3670032
  410.0 6.1 %copy.8 = bf16[2048,896]{1,0:T(8,128)(2,1)} copy(bf16[2048,896]{0,1:T(8,128)(2,1)} %bitcast.14) | data formatting | bytes 7340032
  416.1 1.3 copy-done.3
  417.3 6.5 %convolution_convert_fusion = bf16[296,1792]{1,0:T(8,128)(2,1)} fusion(bf16[2048,296]{0,1:T(8,128)(2,1)S(1)} %copy-done.3, bf16[2048,1792]{1,0:T(8,128)(2,1)} %all-gather.5.cloned.1.call-done), kind=kOutput, calls=%fused_computation.11 | convolution fusion | flops 2173179904 | bytes 9613312 | tf_op jit(solution)/shard_map/dot_general | solution.py:8
  423.9 79.4 %reduce-scatter.5.cloned.1.call-done = bf16[128,896]{1,0:T(8,128)(2,1)} async-done(((bf16[2048,896]{1,0:T(8,128)(2,1)}), bf16[128,896]{1,0:T(8,128)(2,1)}) %reduce-scatter.5.cloned.1.call-update) | async-done | bytes 229392 | tf_op jit(solution)/shard_map/reduce_scatter | solution.py:44
  (90 shorter events, 7.8 us)
Async XLA Ops:
  7.2 349.6 %copy-start = (bf16[296,1792]{1,0:T(8,128)(2,1)S(1)}, bf16[296,1792]{1,0:T(8,128)(2,1)}, u32[]{:S(2)}) copy-start(bf16[296,1792]{1,0:T(8,128)(2,1)} %param.9) | copy-start | bytes 3182596
  7.2 164.7 %copy-start.5 = (bf16[128,896]{1,0:T(8,128)(2,1)S(1)}, bf16[128,896]{1,0:T(8,128)(2,1)}, u32[]{:S(2)}) copy-start(bf16[128,896]{1,0:T(8,128)(2,1)} %param.8) | copy-start | bytes 688132
  7.2 335.6 %all-gather.3.cloned.1.call-start = ((), (), s32[]{:S(2)}) async-start(), calls=%async_computation.2 | async-start | bytes 11010048 | tf_op jit(solution)/shard_map/all_gather | solution.py:30
  7.2 12.8 %collective-permute-start = (bf16[128,896]{1,0:T(8,128)(2,1)}, bf16[128,896]{1,0:T(8,128)(2,1)S(1)}, u32[]{:S(2)}, u32[]{:S(2)}) collective-permute-start(bf16[128,896]{1,0:T(8,128)(2,1)} %param.8), channel_id=1, source_target_pairs={{0,2},{2,4},{4,6},{6,8},{8,10},{10,12},{12,14},{14,16},{16,18},{18... | collective-permute-start | bytes 688136 | tf_op jit(solution)/shard_map/ppermute | solution.py:24
  20.1 10.4 %collective-permute-start.1 = (bf16[128,896]{1,0:T(8,128)(2,1)S(1)}, bf16[128,896]{1,0:T(8,128)(2,1)S(1)}, u32[]{:S(2)}, u32[]{:S(2)}) collective-permute-start(bf16[128,896]{1,0:T(8,128)(2,1)S(1)} %collective-permute-done), channel_id=1, source_target_pairs={{0,2},{2,4},{4,6},{6,8},{8,10},{10,12},{12,14},{14,16},{16,18},{18... | collective-permute-start | bytes 688136 | tf_op jit(solution)/shard_map/ppermute | solution.py:24
  30.4 9.6 %collective-permute-start.2 = (bf16[128,896]{1,0:T(8,128)(2,1)S(1)}, bf16[128,896]{1,0:T(8,128)(2,1)S(1)}, u32[]{:S(2)}, u32[]{:S(2)}) collective-permute-start(bf16[128,896]{1,0:T(8,128)(2,1)S(1)} %collective-permute-done.1), channel_id=1, source_target_pairs={{0,2},{2,4},{4,6},{6,8},{8,10},{10,12},{12,14},{14,16},{16,18},{18... | collective-permute-start | bytes 688136 | tf_op jit(solution)/shard_map/ppermute | solution.py:24
  40.0 9.6 %collective-permute-start.3 = (bf16[128,896]{1,0:T(8,128)(2,1)S(1)}, bf16[128,896]{1,0:T(8,128)(2,1)S(1)}, u32[]{:S(2)}, u32[]{:S(2)}) collective-permute-start(bf16[128,896]{1,0:T(8,128)(2,1)S(1)} %collective-permute-done.2), channel_id=1, source_target_pairs={{0,2},{2,4},{4,6},{6,8},{8,10},{10,12},{12,14},{14,16},{16,18},{18... | collective-permute-start | bytes 688136 | tf_op jit(solution)/shard_map/ppermute | solution.py:24
  49.7 9.6 %collective-permute-start.4 = (bf16[128,896]{1,0:T(8,128)(2,1)S(1)}, bf16[128,896]{1,0:T(8,128)(2,1)S(1)}, u32[]{:S(2)}, u32[]{:S(2)}) collective-permute-start(bf16[128,896]{1,0:T(8,128)(2,1)S(1)} %collective-permute-done.3), channel_id=1, source_target_pairs={{0,2},{2,4},{4,6},{6,8},{8,10},{10,12},{12,14},{14,16},{16,18},{18... | collective-permute-start | bytes 688136 | tf_op jit(solution)/shard_map/ppermute | solution.py:24
  59.3 9.6 %collective-permute-start.5 = (bf16[128,896]{1,0:T(8,128)(2,1)S(1)}, bf16[128,896]{1,0:T(8,128)(2,1)S(1)}, u32[]{:S(2)}, u32[]{:S(2)}) collective-permute-start(bf16[128,896]{1,0:T(8,128)(2,1)S(1)} %collective-permute-done.4), channel_id=1, source_target_pairs={{0,2},{2,4},{4,6},{6,8},{8,10},{10,12},{12,14},{14,16},{16,18},{18... | collective-permute-start | bytes 688136 | tf_op jit(solution)/shard_map/ppermute | solution.py:24
  68.9 10.8 %collective-permute-start.6 = (bf16[128,896]{1,0:T(8,128)(2,1)S(1)}, bf16[128,896]{1,0:T(8,128)(2,1)S(1)}, u32[]{:S(2)}, u32[]{:S(2)}) collective-permute-start(bf16[128,896]{1,0:T(8,128)(2,1)S(1)} %collective-permute-done.5), channel_id=1, source_target_pairs={{0,2},{2,4},{4,6},{6,8},{8,10},{10,12},{12,14},{14,16},{16,18},{18... | collective-permute-start | bytes 688136 | tf_op jit(solution)/shard_map/ppermute | solution.py:24
  79.7 11.9 %collective-permute-start.7 = (bf16[128,896]{1,0:T(8,128)(2,1)S(1)}, bf16[128,896]{1,0:T(8,128)(2,1)S(1)}, u32[]{:S(2)}, u32[]{:S(2)}) collective-permute-start(bf16[128,896]{1,0:T(8,128)(2,1)S(1)} %collective-permute-done.6), channel_id=1, source_target_pairs={{0,2},{2,4},{4,6},{6,8},{8,10},{10,12},{12,14},{14,16},{16,18},{18... | collective-permute-start | bytes 688136 | tf_op jit(solution)/shard_map/ppermute | solution.py:24
  91.6 11.2 %collective-permute-start.8 = (bf16[128,896]{1,0:T(8,128)(2,1)S(1)}, bf16[128,896]{1,0:T(8,128)(2,1)S(1)}, u32[]{:S(2)}, u32[]{:S(2)}) collective-permute-start(bf16[128,896]{1,0:T(8,128)(2,1)S(1)} %collective-permute-done.7), channel_id=1, source_target_pairs={{0,2},{2,4},{4,6},{6,8},{8,10},{10,12},{12,14},{14,16},{16,18},{18... | collective-permute-start | bytes 688136 | tf_op jit(solution)/shard_map/ppermute | solution.py:24
  102.8 11.1 %collective-permute-start.9 = (bf16[128,896]{1,0:T(8,128)(2,1)S(1)}, bf16[128,896]{1,0:T(8,128)(2,1)S(1)}, u32[]{:S(2)}, u32[]{:S(2)}) collective-permute-start(bf16[128,896]{1,0:T(8,128)(2,1)S(1)} %collective-permute-done.8), channel_id=1, source_target_pairs={{0,2},{2,4},{4,6},{6,8},{8,10},{10,12},{12,14},{14,16},{16,18},{18... | collective-permute-start | bytes 688136 | tf_op jit(solution)/shard_map/ppermute | solution.py:24
  113.9 0.7 copy-start.7
  114.6 10.2 %collective-permute-start.10 = (bf16[128,896]{1,0:T(8,128)(2,1)S(1)}, bf16[128,896]{1,0:T(8,128)(2,1)S(1)}, u32[]{:S(2)}, u32[]{:S(2)}) collective-permute-start(bf16[128,896]{1,0:T(8,128)(2,1)S(1)} %collective-permute-done.9), channel_id=1, source_target_pairs={{0,2},{2,4},{4,6},{6,8},{8,10},{10,12},{12,14},{14,16},{16,18},{18... | collective-permute-start | bytes 688136 | tf_op jit(solution)/shard_map/ppermute | solution.py:24
  124.8 0.7 copy-start.8
  125.5 9.6 %collective-permute-start.11 = (bf16[128,896]{1,0:T(8,128)(2,1)S(1)}, bf16[128,896]{1,0:T(8,128)(2,1)S(1)}, u32[]{:S(2)}, u32[]{:S(2)}) collective-permute-start(bf16[128,896]{1,0:T(8,128)(2,1)S(1)} %collective-permute-done.10), channel_id=1, source_target_pairs={{0,2},{2,4},{4,6},{6,8},{8,10},{10,12},{12,14},{14,16},{16,18},{18... | collective-permute-start | bytes 688136 | tf_op jit(solution)/shard_map/ppermute | solution.py:24
  135.1 0.7 copy-start.9
  135.8 9.6 %collective-permute-start.12 = (bf16[128,896]{1,0:T(8,128)(2,1)S(1)}, bf16[128,896]{1,0:T(8,128)(2,1)S(1)}, u32[]{:S(2)}, u32[]{:S(2)}) collective-permute-start(bf16[128,896]{1,0:T(8,128)(2,1)S(1)} %collective-permute-done.11), channel_id=1, source_target_pairs={{0,2},{2,4},{4,6},{6,8},{8,10},{10,12},{12,14},{14,16},{16,18},{18... | collective-permute-start | bytes 688136 | tf_op jit(solution)/shard_map/ppermute | solution.py:24
  145.4 0.7 copy-start.10
  146.1 9.7 %collective-permute-start.13 = (bf16[128,896]{1,0:T(8,128)(2,1)S(1)}, bf16[128,896]{1,0:T(8,128)(2,1)}, u32[]{:S(2)}, u32[]{:S(2)}) collective-permute-start(bf16[128,896]{1,0:T(8,128)(2,1)S(1)} %collective-permute-done.12), channel_id=1, source_target_pairs={{0,2},{2,4},{4,6},{6,8},{8,10},{10,12},{12,14},{14,16},{16,18},{18... | collective-permute-start | bytes 688136 | tf_op jit(solution)/shard_map/ppermute | solution.py:24
  155.8 9.9 %collective-permute-start.14 = (bf16[128,896]{1,0:T(8,128)(2,1)}, bf16[128,896]{1,0:T(8,128)(2,1)}, u32[]{:S(2)}, u32[]{:S(2)}) collective-permute-start(bf16[128,896]{1,0:T(8,128)(2,1)} %collective-permute-done.13), channel_id=1, source_target_pairs={{0,2},{2,4},{4,6},{6,8},{8,10},{10,12},{12,14},{14,16},{16,18},{18... | collective-permute-start | bytes 688136 | tf_op jit(solution)/shard_map/ppermute | solution.py:24
  179.1 0.9 copy-start.6
  179.1 177.6 %all-gather.5.cloned.1.call-start = ((), (), s32[]{:S(2)}) async-start(), calls=%async_computation.3 | async-start | bytes 11010048 | tf_op jit(solution)/shard_map/all_gather | solution.py:30
  180.0 11.6 %collective-permute-start.15 = (bf16[128,896]{1,0:T(8,128)(2,1)S(1)}, bf16[128,896]{1,0:T(8,128)(2,1)S(1)}, u32[]{:S(2)}, u32[]{:S(2)}) collective-permute-start(bf16[128,896]{1,0:T(8,128)(2,1)S(1)} %copy-done.6), channel_id=1, source_target_pairs={{0,2},{2,4},{4,6},{6,8},{8,10},{10,12},{12,14},{14,16},{16,18},{18... | collective-permute-start | bytes 688136 | tf_op jit(solution)/shard_map/ppermute | solution.py:24
  191.7 11.4 %collective-permute-start.16 = (bf16[128,896]{1,0:T(8,128)(2,1)S(1)}, bf16[128,896]{1,0:T(8,128)(2,1)S(1)}, u32[]{:S(2)}, u32[]{:S(2)}) collective-permute-start(bf16[128,896]{1,0:T(8,128)(2,1)S(1)} %collective-permute-done.15), channel_id=1, source_target_pairs={{0,2},{2,4},{4,6},{6,8},{8,10},{10,12},{12,14},{14,16},{16,18},{18... | collective-permute-start | bytes 688136 | tf_op jit(solution)/shard_map/ppermute | solution.py:24
  203.0 10.5 %collective-permute-start.17 = (bf16[128,896]{1,0:T(8,128)(2,1)S(1)}, bf16[128,896]{1,0:T(8,128)(2,1)S(1)}, u32[]{:S(2)}, u32[]{:S(2)}) collective-permute-start(bf16[128,896]{1,0:T(8,128)(2,1)S(1)} %collective-permute-done.16), channel_id=1, source_target_pairs={{0,2},{2,4},{4,6},{6,8},{8,10},{10,12},{12,14},{14,16},{16,18},{18... | collective-permute-start | bytes 688136 | tf_op jit(solution)/shard_map/ppermute | solution.py:24
  213.6 9.7 %collective-permute-start.18 = (bf16[128,896]{1,0:T(8,128)(2,1)S(1)}, bf16[128,896]{1,0:T(8,128)(2,1)S(1)}, u32[]{:S(2)}, u32[]{:S(2)}) collective-permute-start(bf16[128,896]{1,0:T(8,128)(2,1)S(1)} %collective-permute-done.17), channel_id=1, source_target_pairs={{0,2},{2,4},{4,6},{6,8},{8,10},{10,12},{12,14},{14,16},{16,18},{18... | collective-permute-start | bytes 688136 | tf_op jit(solution)/shard_map/ppermute | solution.py:24
  223.2 9.6 %collective-permute-start.19 = (bf16[128,896]{1,0:T(8,128)(2,1)S(1)}, bf16[128,896]{1,0:T(8,128)(2,1)S(1)}, u32[]{:S(2)}, u32[]{:S(2)}) collective-permute-start(bf16[128,896]{1,0:T(8,128)(2,1)S(1)} %collective-permute-done.18), channel_id=1, source_target_pairs={{0,2},{2,4},{4,6},{6,8},{8,10},{10,12},{12,14},{14,16},{16,18},{18... | collective-permute-start | bytes 688136 | tf_op jit(solution)/shard_map/ppermute | solution.py:24
  232.8 9.6 %collective-permute-start.20 = (bf16[128,896]{1,0:T(8,128)(2,1)S(1)}, bf16[128,896]{1,0:T(8,128)(2,1)S(1)}, u32[]{:S(2)}, u32[]{:S(2)}) collective-permute-start(bf16[128,896]{1,0:T(8,128)(2,1)S(1)} %collective-permute-done.19), channel_id=1, source_target_pairs={{0,2},{2,4},{4,6},{6,8},{8,10},{10,12},{12,14},{14,16},{16,18},{18... | collective-permute-start | bytes 688136 | tf_op jit(solution)/shard_map/ppermute | solution.py:24
  242.5 9.6 %collective-permute-start.21 = (bf16[128,896]{1,0:T(8,128)(2,1)S(1)}, bf16[128,896]{1,0:T(8,128)(2,1)S(1)}, u32[]{:S(2)}, u32[]{:S(2)}) collective-permute-start(bf16[128,896]{1,0:T(8,128)(2,1)S(1)} %collective-permute-done.20), channel_id=1, source_target_pairs={{0,2},{2,4},{4,6},{6,8},{8,10},{10,12},{12,14},{14,16},{16,18},{18... | collective-permute-start | bytes 688136 | tf_op jit(solution)/shard_map/ppermute | solution.py:24
  252.1 10.3 %collective-permute-start.22 = (bf16[128,896]{1,0:T(8,128)(2,1)S(1)}, bf16[128,896]{1,0:T(8,128)(2,1)S(1)}, u32[]{:S(2)}, u32[]{:S(2)}) collective-permute-start(bf16[128,896]{1,0:T(8,128)(2,1)S(1)} %collective-permute-done.21), channel_id=1, source_target_pairs={{0,2},{2,4},{4,6},{6,8},{8,10},{10,12},{12,14},{14,16},{16,18},{18... | collective-permute-start | bytes 688136 | tf_op jit(solution)/shard_map/ppermute | solution.py:24
  262.4 11.5 %collective-permute-start.23 = (bf16[128,896]{1,0:T(8,128)(2,1)S(1)}, bf16[128,896]{1,0:T(8,128)(2,1)S(1)}, u32[]{:S(2)}, u32[]{:S(2)}) collective-permute-start(bf16[128,896]{1,0:T(8,128)(2,1)S(1)} %collective-permute-done.22), channel_id=1, source_target_pairs={{0,2},{2,4},{4,6},{6,8},{8,10},{10,12},{12,14},{14,16},{16,18},{18... | collective-permute-start | bytes 688136 | tf_op jit(solution)/shard_map/ppermute | solution.py:24
  273.9 11.5 %collective-permute-start.24 = (bf16[128,896]{1,0:T(8,128)(2,1)S(1)}, bf16[128,896]{1,0:T(8,128)(2,1)S(1)}, u32[]{:S(2)}, u32[]{:S(2)}) collective-permute-start(bf16[128,896]{1,0:T(8,128)(2,1)S(1)} %collective-permute-done.23), channel_id=1, source_target_pairs={{0,2},{2,4},{4,6},{6,8},{8,10},{10,12},{12,14},{14,16},{16,18},{18... | collective-permute-start | bytes 688136 | tf_op jit(solution)/shard_map/ppermute | solution.py:24
  285.4 10.7 %collective-permute-start.25 = (bf16[128,896]{1,0:T(8,128)(2,1)S(1)}, bf16[128,896]{1,0:T(8,128)(2,1)S(1)}, u32[]{:S(2)}, u32[]{:S(2)}) collective-permute-start(bf16[128,896]{1,0:T(8,128)(2,1)S(1)} %collective-permute-done.24), channel_id=1, source_target_pairs={{0,2},{2,4},{4,6},{6,8},{8,10},{10,12},{12,14},{14,16},{16,18},{18... | collective-permute-start | bytes 688136 | tf_op jit(solution)/shard_map/ppermute | solution.py:24
  296.1 9.8 %collective-permute-start.26 = (bf16[128,896]{1,0:T(8,128)(2,1)S(1)}, bf16[128,896]{1,0:T(8,128)(2,1)S(1)}, u32[]{:S(2)}, u32[]{:S(2)}) collective-permute-start(bf16[128,896]{1,0:T(8,128)(2,1)S(1)} %collective-permute-done.25), channel_id=1, source_target_pairs={{0,2},{2,4},{4,6},{6,8},{8,10},{10,12},{12,14},{14,16},{16,18},{18... | collective-permute-start | bytes 688136 | tf_op jit(solution)/shard_map/ppermute | solution.py:24
  305.9 9.6 %collective-permute-start.27 = (bf16[128,896]{1,0:T(8,128)(2,1)S(1)}, bf16[128,896]{1,0:T(8,128)(2,1)S(1)}, u32[]{:S(2)}, u32[]{:S(2)}) collective-permute-start(bf16[128,896]{1,0:T(8,128)(2,1)S(1)} %collective-permute-done.26), channel_id=1, source_target_pairs={{0,2},{2,4},{4,6},{6,8},{8,10},{10,12},{12,14},{14,16},{16,18},{18... | collective-permute-start | bytes 688136 | tf_op jit(solution)/shard_map/ppermute | solution.py:24
  315.5 9.6 %collective-permute-start.28 = (bf16[128,896]{1,0:T(8,128)(2,1)S(1)}, bf16[128,896]{1,0:T(8,128)(2,1)S(1)}, u32[]{:S(2)}, u32[]{:S(2)}) collective-permute-start(bf16[128,896]{1,0:T(8,128)(2,1)S(1)} %collective-permute-done.27), channel_id=1, source_target_pairs={{0,2},{2,4},{4,6},{6,8},{8,10},{10,12},{12,14},{14,16},{16,18},{18... | collective-permute-start | bytes 688136 | tf_op jit(solution)/shard_map/ppermute | solution.py:24
  325.1 9.6 %collective-permute-start.29 = (bf16[128,896]{1,0:T(8,128)(2,1)S(1)}, bf16[128,896]{1,0:T(8,128)(2,1)S(1)}, u32[]{:S(2)}, u32[]{:S(2)}) collective-permute-start(bf16[128,896]{1,0:T(8,128)(2,1)S(1)} %collective-permute-done.28), channel_id=1, source_target_pairs={{0,2},{2,4},{4,6},{6,8},{8,10},{10,12},{12,14},{14,16},{16,18},{18... | collective-permute-start | bytes 688136 | tf_op jit(solution)/shard_map/ppermute | solution.py:24
  342.5 67.5 %reduce-scatter.7.cloned.1.call-start = ((), (), s32[]{:S(2)}) async-start(), calls=%async_computation.5 | async-start | bytes 11010048
  356.7 5.6 %copy-start.4 = (bf16[296,1792]{1,0:T(8,128)(2,1)S(1)}, bf16[296,1792]{1,0:T(8,128)(2,1)}, u32[]{:S(2)}) copy-start(bf16[296,1792]{1,0:T(8,128)(2,1)} %param.10) | copy-start | bytes 3182596
  356.7 5.6 %copy-start.11 = (bf16[2048,1792]{1,0:T(8,128)(2,1)S(1)}, bf16[2048,1792]{1,0:T(8,128)(2,1)}, u32[]{:S(2)}) copy-start(bf16[2048,1792]{1,0:T(8,128)(2,1)} %all-gather.5.cloned.1.call-done) | copy-start | bytes 22020100
  365.2 7.4 %copy-start.2 = (bf16[2048,296]{0,1:T(8,128)(2,1)}, bf16[2048,296]{0,1:T(8,128)(2,1)S(1)}, u32[]{:S(2)}) copy-start(bf16[2048,296]{0,1:T(8,128)(2,1)S(1)} %fusion.4) | copy-start | bytes 3637252
  392.5 110.7 %reduce-scatter.5.cloned.1.call-start = ((), (), s32[]{:S(2)}) async-start(), calls=%async_computation.4 | async-start | bytes 3899392 | tf_op jit(solution)/shard_map/reduce_scatter | solution.py:44
  416.0 1.3 copy-start.3
  417.3 85.9 %copy-start.1 = (bf16[296,1792]{1,0:T(8,128)(2,1)S(1)}, bf16[296,1792]{1,0:T(8,128)(2,1)}, u32[]{:S(2)}) copy-start(bf16[296,1792]{1,0:T(8,128)(2,1)} %param.9) | copy-start | bytes 3182596
Sparse Core Ops, SparseCore 0:
  179.3 14.0 all-gather.2
  342.6 14.0 all-gather.4
  392.6 17.3 reduce-scatter.6
  416.2 86.9 reduce-scatter.4
